TPU v7x, 32 devices: a whole 2x2x4 slice. The times are simulated.
32 devices in a mesh: blk: 16 (over z, y, core), row: 2 (over x).
Axes of the slice: x: 2, y: 2, z: 4, core: 2. Of those that a mesh axis runs over, the one named last changes fastest.
Arguments:
- features: float32 [2048, 256], P(('blk', 'row')), may hold values from -2 to 2, as said below
- probes: float32 [2048, 128], P(('blk', 'row')), may hold values from -6 to 6
- outputscale: float32 [1], replicated, may hold values from 0.05 to 0.2
- noise: float32 [1], replicated, may hold values from 0.5 to 2
- pivots: int32 [256], replicated, may hold values from 0 to 2047, as said below
Outputs:
- product: float32 [2048, 128], P(('blk', 'row'))
- preconditioned: float32 [2048, 128], P(('blk', 'row'))
Inputs may be any that keep to these rules, and one draw needn't show every extreme that they name: `pivots`: 256 distinct point indices. real-valued features.
All inputs are finite; a program needn't handle non-finite values.
Results may differ from a plain program's by a relative error of at most 0.0003.
Values sent between devices are 32-bit elements; how exact they have to be, the bound alone decides.
No kernel may reach another device: no remote copies, remote signals or barrier semaphores. Data moves between devices by JAX's collectives and lax.ppermute only.
A program may use at most 64 MiB of HBM per device.

v0:
```python
import jax
import jax.numpy as jnp
from jax import lax
from jax.sharding import PartitionSpec as P

STRIDE = 4
highest = lax.Precision.HIGHEST
root_five = 2.23606797749979


def shifted(block, axis, distance):
    devices = range(lax.axis_size(axis))
    route = [((i - distance) % len(devices), i) for i in devices]
    return lax.ppermute(block, axis, route)


def kernel_tile(row_feats, row_norms, col_feats, col_norms):
    inner = lax.dot_general(
        row_feats,
        col_feats,
        (((1,), (1,)), ((), ())),
        precision=highest,
        preferred_element_type=jnp.float32,
    )
    squared = jnp.maximum(row_norms[:, None] + col_norms[None, :] - 2.0 * inner, 0.0)
    scaled = root_five * jnp.sqrt(squared)
    return (1.0 + scaled + scaled * scaled / 3.0) * jnp.exp(-scaled)


def transposed_product(kernel_block, row_probes):
    return lax.dot_general(
        kernel_block,
        row_probes,
        (((0,), (0,)), ((), ())),
        precision=highest,
        preferred_element_type=jnp.float32,
    )


def quorum_members(block_count, spacing):
    half_count = block_count // 2
    members = list(range(spacing))
    reached = 0
    while reached < half_count:
        reached = reached + spacing
        members.append(reached % block_count)
    return members


def quorum_pairs(block_count, members):
    pair_list = []
    for offset in range(block_count // 2 + 1):
        chosen = None
        for lower_slot, lower_member in enumerate(members):
            for upper_slot, upper_member in enumerate(members):
                if chosen is None and (upper_member - lower_member) % block_count == offset:
                    chosen = (lower_slot, upper_slot)
        two_sided = offset != 0 and 2 * offset != block_count
        pair_list.append((chosen[0], chosen[1], two_sided))
    return pair_list


def member_sweep(fetched, fetched_norms, upper, lower_group, block_rows):
    local_rows, probe_count = fetched[upper][1].shape
    column_sums = jnp.zeros((block_rows, probe_count), jnp.float32)
    arrived_feats = lax.all_gather(fetched[upper][0], "row", axis=0, tiled=True)
    arrived_probes = lax.all_gather(fetched[upper][1], "row", axis=0, tiled=True)
    arrived_norms = jnp.sum(arrived_feats * arrived_feats, axis=1)
    updated = []
    for position, (lower, two_sided) in enumerate(lower_group):
        kernel_block = kernel_tile(
            fetched[lower][0], fetched_norms[lower], arrived_feats, arrived_norms
        )
        updated.append(
            jnp.dot(
                kernel_block, arrived_probes, precision=highest, preferred_element_type=jnp.float32
            )
        )
        if two_sided:
            current = column_sums
            column_sums = current + transposed_product(kernel_block, fetched[lower][1])
    return (tuple(updated), column_sums)


def per_device(features, probes, outputscale, noise, pivots):
    local_rows, probe_count = probes.shape
    block_count = lax.axis_size("blk")
    piece_count = lax.axis_size("row")
    piece_index = lax.axis_index("row")
    amplitude = outputscale[0]
    nugget = noise[0]
    members = quorum_members(block_count, STRIDE)
    pair_list = quorum_pairs(block_count, members)
    slot_count = len(members)
    block_rows = local_rows * piece_count
    own_norms = jnp.sum(features * features, axis=1)
    forward = [jnp.zeros((local_rows, probe_count), jnp.float32) for member in members]
    backward = [jnp.zeros((block_rows, probe_count), jnp.float32) for member in members]
    fetched = [(features, probes)]
    for member in members[1:]:
        fetched.append(shifted((features, probes), "blk", block_count - member))
    fetched_norms = [jnp.sum(entry[0] * entry[0], axis=1) for entry in fetched]
    for upper in range(slot_count):
        lower_group = [
            (lower, two_sided) for lower, target, two_sided in pair_list if target == upper
        ]
        partials, column_sums = member_sweep(fetched, fetched_norms, upper, lower_group, block_rows)
        for position, (lower, two_sided) in enumerate(lower_group):
            forward[lower] = forward[lower] + partials[position]
        backward[upper] = column_sums
    shared = lax.psum_scatter(jnp.stack(backward), "row", scatter_dimension=1, tiled=True)
    kernel_probes = forward[0] + shared[0]
    for position in range(1, slot_count):
        outgoing = forward[position] + shared[position]
        kernel_probes = kernel_probes + shifted(outgoing, "blk", members[position])
    product = amplitude * kernel_probes + nugget * probes
    flat_index = lax.axis_index("blk") * piece_count + piece_index
    offsets = pivots - flat_index * local_rows
    inside = (offsets >= 0) & (offsets < local_rows)
    picked = jnp.where(inside[:, None], features[jnp.clip(offsets, 0, local_rows - 1)], 0.0)
    pivot_feats = lax.psum(picked, ("blk", "row"))
    pivot_norms = jnp.sum(pivot_feats * pivot_feats, axis=1)
    cross = amplitude * kernel_tile(features, own_norms, pivot_feats, pivot_norms)
    gram_part = lax.dot_general(
        cross,
        cross,
        (((0,), (0,)), ((), ())),
        precision=highest,
        preferred_element_type=jnp.float32,
    )
    projected_part = lax.dot_general(
        cross,
        product,
        (((0,), (0,)), ((), ())),
        precision=highest,
        preferred_element_type=jnp.float32,
    )
    gram_sum, projected = lax.psum((gram_part, projected_part), ("blk", "row"))
    inner_pivots = amplitude * kernel_tile(pivot_feats, pivot_norms, pivot_feats, pivot_norms)
    gram = nugget * inner_pivots + gram_sum
    factor = jnp.linalg.cholesky(gram)
    coefficients = jax.scipy.linalg.cho_solve((factor, True), projected)
    preconditioned = (
        product
        - jnp.dot(cross, coefficients, precision=highest, preferred_element_type=jnp.float32)
    ) / nugget
    return (product, preconditioned)


def solution(mesh):
    in_specs = (P(("blk", "row"), None), P(("blk", "row"), None), P(), P(), P())
    out_specs = (P(("blk", "row"), None), P(("blk", "row"), None))
    return jax.shard_map(
        per_device, mesh=mesh, in_specs=in_specs, out_specs=out_specs, check_vma=False
    )
```

profile of v0, /device:TPU:0, one launch (start us, length us, event | category | flops | bytes accessed | tf_op | source)
XLA Modules:
  0.0 363.2 jit_solution(4064739874456005614)
XLA Ops:
  8.0 5.5 %collective-permute-start = (f32[64,256]{1,0:T(8,128)}, f32[64,256]{1,0:T(8,128)S(1)}, u32[]{:S(2)}, u32[]{:S(2)}) collective-permute-start(f32[64,256]{1,0:T(8,128)} %param.5), channel_id=1, source_target_pairs={{2,0},{4,2},{6,4},{8,6},{10,8},{12,10},{14,12},{16,14},{18,16},{20... | collective-permute-start | bytes 196616 | tf_op jit(solution)/shard_map/ppermute | solution.py:14
  14.4 1.4 collective-permute-start.1
  16.5 1.8 gather_fusion
  20.2 5.1 %all_gather.36 = f32[128,256]{1,0:T(8,128)S(1)} all-gather(f32[64,256]{1,0:T(8,128)S(1)} %copy-done), channel_id=1, replica_groups=mesh['blk'=16,'row'=2] {'row'}, dimensions={0}, use_global_device_ids=true | all-gather | bytes 196608 | tf_op jit(solution)/shard_map/all_gather | solution.py:66
  25.2 4.6 %all_gather.37 = f32[128,128]{1,0:T(8,128)S(1)} all-gather(f32[64,128]{1,0:T(8,128)S(1)} %copy-done.1), channel_id=1, replica_groups=mesh['blk'=16,'row'=2] {'row'}, dimensions={0}, use_global_device_ids=true | all-gather | bytes 98304 | tf_op jit(solution)/shard_map/all_gather | solution.py:67
  32.5 4.6 %all_gather.47 = f32[128,128]{1,0:T(8,128)S(1)} all-gather(f32[64,128]{1,0:T(8,128)S(1)} %collective-permute-done.9), channel_id=1, replica_groups=mesh['blk'=16,'row'=2] {'row'}, dimensions={0}, use_global_device_ids=true | all-gather | bytes 98304 | tf_op jit(solution)/shard_map/all_gather | solution.py:67
  37.1 3.2 collective-permute-start.7
  40.3 4.6 %all_gather.39 = f32[128,128]{1,0:T(8,128)S(1)} all-gather(f32[64,128]{1,0:T(8,128)S(1)} %collective-permute-done.1), channel_id=1, replica_groups=mesh['blk'=16,'row'=2] {'row'}, dimensions={0}, use_global_device_ids=true | all-gather | bytes 98304 | tf_op jit(solution)/shard_map/all_gather | solution.py:67
  44.9 1.4 collective-permute-start.3
  46.3 4.6 %all_gather.43 = f32[128,128]{1,0:T(8,128)S(1)} all-gather(f32[64,128]{1,0:T(8,128)S(1)} %collective-permute-done.5), channel_id=1, replica_groups=mesh['blk'=16,'row'=2] {'row'}, dimensions={0}, use_global_device_ids=true | all-gather | bytes 98304 | tf_op jit(solution)/shard_map/all_gather | solution.py:67
  51.0 4.6 %all_gather.45 = f32[128,128]{1,0:T(8,128)S(1)} all-gather(f32[64,128]{1,0:T(8,128)S(1)} %collective-permute-done.7), channel_id=1, replica_groups=mesh['blk'=16,'row'=2] {'row'}, dimensions={0}, use_global_device_ids=true | all-gather | bytes 98304 | tf_op jit(solution)/shard_map/all_gather | solution.py:67
  55.5 3.0 collective-permute-start.8
  58.5 4.6 %all_gather.41 = f32[128,128]{1,0:T(8,128)S(1)} all-gather(f32[64,128]{1,0:T(8,128)S(1)} %collective-permute-done.3), channel_id=1, replica_groups=mesh['blk'=16,'row'=2] {'row'}, dimensions={0}, use_global_device_ids=true | all-gather | bytes 98304 | tf_op jit(solution)/shard_map/all_gather | solution.py:67
  63.1 4.9 %all_gather.38 = f32[128,256]{1,0:T(8,128)S(1)} all-gather(f32[64,256]{1,0:T(8,128)S(1)} %collective-permute-done), channel_id=1, replica_groups=mesh['blk'=16,'row'=2] {'row'}, dimensions={0}, use_global_device_ids=true | all-gather | bytes 196608 | tf_op jit(solution)/shard_map/all_gather | solution.py:66
  68.4 5.0 %all_gather.40 = f32[128,256]{1,0:T(8,128)S(1)} all-gather(f32[64,256]{1,0:T(8,128)S(1)} %collective-permute-done.2), channel_id=1, replica_groups=mesh['blk'=16,'row'=2] {'row'}, dimensions={0}, use_global_device_ids=true | all-gather | bytes 196608 | tf_op jit(solution)/shard_map/all_gather | solution.py:66
  73.9 5.6 %all_gather.42 = f32[128,256]{1,0:T(8,128)S(1)} all-gather(f32[64,256]{1,0:T(8,128)S(1)} %collective-permute-done.4), channel_id=1, replica_groups=mesh['blk'=16,'row'=2] {'row'}, dimensions={0}, use_global_device_ids=true | all-gather | bytes 196608 | tf_op jit(solution)/shard_map/all_gather | solution.py:66
  79.9 4.9 %all_gather.46 = f32[128,256]{1,0:T(8,128)S(1)} all-gather(f32[64,256]{1,0:T(8,128)S(1)} %collective-permute-done.8), channel_id=1, replica_groups=mesh['blk'=16,'row'=2] {'row'}, dimensions={0}, use_global_device_ids=true | all-gather | bytes 196608 | tf_op jit(solution)/shard_map/all_gather | solution.py:66
  85.2 4.9 %all_gather.44 = f32[128,256]{1,0:T(8,128)S(1)} all-gather(f32[64,256]{1,0:T(8,128)S(1)} %collective-permute-done.6), channel_id=1, replica_groups=mesh['blk'=16,'row'=2] {'row'}, dimensions={0}, use_global_device_ids=true | all-gather | bytes 196608 | tf_op jit(solution)/shard_map/all_gather | solution.py:66
  95.3 52.4 %all-reduce.5.cloned.1.call-done = f32[256,256]{0,1:T(8,128)} async-done(((f32[256,256]{0,1:T(8,128)}), f32[256,256]{0,1:T(8,128)}) %all-reduce.5.cloned.1.call-update) | async-done | bytes 262160 | tf_op jit(solution)/shard_map/psum | solution.py:121
  151.2 1.5 collective-permute-start.11
  152.9 2.4 collective-permute-start.12
  155.9 2.4 collective-permute-start.14
  159.4 1.7 collective-permute-done.13
  162.4 128.9 %all-reduce.7.cloned.1.call-done = (f32[256,128]{1,0:T(8,128)}, f32[256,256]{0,1:T(8,128)}) async-done(((f32[256,128]{1,0:T(8,128)}, f32[256,256]{0,1:T(8,128)}), (f32[256,128]{1,0:T(8,128)}, f32[256,256]{0,1:T(8,128)})) %all-reduce.7.cloned.1.call-update) | async-done | bytes 393232 | tf_op jit(solution)/shard_map/psum | solution.py:138
  291.3 1.7 multiply_add_fusion
  293.2 11.7 %cholesky.49 = f32[128,128]{1,0:T(8,128)S(1)} custom-call(f32[128,128]{1,0:T(8,128)S(1)} %cholesky.115), custom_call_target="Cholesky" | custom-call | tf_op jit(solution)/shard_map/jit(cholesky)/cholesky | solution.py:141
  304.9 9.8 %custom-call.18 = f32[1,128,128]{1,2,0:T(8,128)S(1)} custom-call(f32[1,128,128]{2,1,0:T(8,128)S(1)} %get-tuple-element.29), custom_call_target="InvertDiagBlocksLowerTriangular" | custom-call | tf_op jit(solution)/shard_map/jit(cholesky)/cholesky | solution.py:141
  315.2 11.7 %cholesky.103 = f32[128,128]{1,0:T(8,128)S(1)} custom-call(f32[128,128]{1,0:T(8,128)S(1)} %convolution_subtract_fusion.2), custom_call_target="Cholesky" | custom-call | tf_op jit(solution)/shard_map/jit(cholesky)/cholesky | solution.py:141
  329.4 4.4 %while.1 = (s32[]{:T(128)}, f32[256,256]{0,1:T(8,128)S(1)}, s32[2,2]{1,0:T(2,128)S(1)}, f32[2,128,128]{2,1,0:T(8,128)S(1)}, s32[]{:T(128)}) while((s32[]{:T(128)}, f32[256,256]{0,1:T(8,128)S(1)}, s32[2,2]{1,0:T(2,128)S(1)}, f32[2,128,128]{2,1,0:T(8,128)S(1)}, s32[]{:T(128)}) %tuple.27), condition=%wide.while_cond, body=%wide.while_body.sunk | while | flops 2 | bytes 393321 | solution.py:142
  330.1 1.4 dynamic-slice.7
  332.2 1.4 dynamic-slice.7
  333.7 19.7 %custom-call.19 = f32[2,128,128]{1,2,0:T(8,128)S(1)} custom-call(f32[2,128,128]{2,1,0:T(8,128)S(1)} %get-tuple-element.9), custom_call_target="InvertDiagBlocksLowerTriangular" | custom-call | tf_op jit(solution)/shard_map/jit(_cho_solve)/triangular_solve | solution.py:142
  (123 shorter events, 23.5 us)
Async XLA Ops:
  8.0 139.7 %all-reduce.5.cloned.1.call-start = ((), (), s32[]{:S(2)}) async-start(), calls=%async_computation.2 | async-start | bytes 524288 | tf_op jit(solution)/shard_map/psum | solution.py:121
  8.0 55.0 %collective-permute-start = (f32[64,256]{1,0:T(8,128)}, f32[64,256]{1,0:T(8,128)S(1)}, u32[]{:S(2)}, u32[]{:S(2)}) collective-permute-start(f32[64,256]{1,0:T(8,128)} %param.5), channel_id=1, source_target_pairs={{2,0},{4,2},{6,4},{8,6},{10,8},{12,10},{14,12},{16,14},{18,16},{20... | collective-permute-start | bytes 196616 | tf_op jit(solution)/shard_map/ppermute | solution.py:14
  13.6 54.8 %collective-permute-start.2 = (f32[64,256]{1,0:T(8,128)}, f32[64,256]{1,0:T(8,128)S(1)}, u32[]{:S(2)}, u32[]{:S(2)}) collective-permute-start(f32[64,256]{1,0:T(8,128)} %param.5), channel_id=1, source_target_pairs={{4,0},{6,2},{8,4},{10,6},{12,8},{14,10},{16,12},{18,14},{20,16},{2... | collective-permute-start | bytes 196616 | tf_op jit(solution)/shard_map/ppermute | solution.py:14
  14.2 59.7 %collective-permute-start.4 = (f32[64,256]{1,0:T(8,128)}, f32[64,256]{1,0:T(8,128)S(1)}, u32[]{:S(2)}, u32[]{:S(2)}) collective-permute-start(f32[64,256]{1,0:T(8,128)} %param.5), channel_id=1, source_target_pairs={{6,0},{8,2},{10,4},{12,6},{14,8},{16,10},{18,12},{20,14},{22,16},{... | collective-permute-start | bytes 196616 | tf_op jit(solution)/shard_map/ppermute | solution.py:14
  14.4 22.7 %collective-permute-start.1 = (f32[64,128]{1,0:T(8,128)}, f32[64,128]{1,0:T(8,128)S(1)}, u32[]{:S(2)}, u32[]{:S(2)}) collective-permute-start(f32[64,128]{1,0:T(8,128)} %param.6), channel_id=1, source_target_pairs={{2,0},{4,2},{6,4},{8,6},{10,8},{12,10},{14,12},{16,14},{18,16},{20... | collective-permute-start | bytes 98312 | tf_op jit(solution)/shard_map/ppermute | solution.py:14
  15.8 15.9 %collective-permute-start.9 = (f32[64,128]{1,0:T(8,128)}, f32[64,128]{1,0:T(8,128)S(1)}, u32[]{:S(2)}, u32[]{:S(2)}) collective-permute-start(f32[64,128]{1,0:T(8,128)} %param.6), channel_id=1, source_target_pairs={{16,0},{18,2},{20,4},{22,6},{24,8},{26,10},{28,12},{30,14},{0,16},... | collective-permute-start | bytes 98312 | tf_op jit(solution)/shard_map/ppermute | solution.py:14
  15.8 0.7 copy-start.7
  19.2 0.8 copy-start
  19.2 129.9 %reduce-scatter.2.cloned.1.call-start = ((), (), s32[]{:S(2)}) async-start(), calls=%async_computation.1 | async-start | bytes 589824 | tf_op jit(solution)/shard_map/reduce_scatter | solution.py:111
  20.2 5.1 %copy-start.1 = (f32[64,128]{1,0:T(8,128)S(1)}, f32[64,128]{1,0:T(8,128)}, u32[]{:S(2)}) copy-start(f32[64,128]{1,0:T(8,128)} %param.6) | copy-start | bytes 98308
  31.7 13.2 %collective-permute-start.5 = (f32[64,128]{1,0:T(8,128)S(1)}, f32[64,128]{1,0:T(8,128)S(1)}, u32[]{:S(2)}, u32[]{:S(2)}) collective-permute-start(f32[64,128]{1,0:T(8,128)S(1)} %copy-done.1), channel_id=1, source_target_pairs={{6,0},{8,2},{10,4},{12,6},{14,8},{16,10},{18,12},{20,14},{22,16},{... | collective-permute-start | bytes 98312 | tf_op jit(solution)/shard_map/ppermute | solution.py:14
  37.1 13.8 %collective-permute-start.7 = (f32[64,128]{1,0:T(8,128)S(1)}, f32[64,128]{1,0:T(8,128)S(1)}, u32[]{:S(2)}, u32[]{:S(2)}) collective-permute-start(f32[64,128]{1,0:T(8,128)S(1)} %copy-done.1), channel_id=1, source_target_pairs={{8,0},{10,2},{12,4},{14,6},{16,8},{18,10},{20,12},{22,14},{24,16},... | collective-permute-start | bytes 98312 | tf_op jit(solution)/shard_map/ppermute | solution.py:14
  44.9 10.7 %collective-permute-start.3 = (f32[64,128]{1,0:T(8,128)S(1)}, f32[64,128]{1,0:T(8,128)S(1)}, u32[]{:S(2)}, u32[]{:S(2)}) collective-permute-start(f32[64,128]{1,0:T(8,128)S(1)} %copy-done.1), channel_id=1, source_target_pairs={{4,0},{6,2},{8,4},{10,6},{12,8},{14,10},{16,12},{18,14},{20,16},{2... | collective-permute-start | bytes 98312 | tf_op jit(solution)/shard_map/ppermute | solution.py:14
  50.9 34.3 %collective-permute-start.6 = (f32[64,256]{1,0:T(8,128)S(1)}, f32[64,256]{1,0:T(8,128)S(1)}, u32[]{:S(2)}, u32[]{:S(2)}) collective-permute-start(f32[64,256]{1,0:T(8,128)S(1)} %copy-done), channel_id=1, source_target_pairs={{8,0},{10,2},{12,4},{14,6},{16,8},{18,10},{20,12},{22,14},{24,16},... | collective-permute-start | bytes 196616 | tf_op jit(solution)/shard_map/ppermute | solution.py:14
  55.5 24.4 %collective-permute-start.8 = (f32[64,256]{1,0:T(8,128)S(1)}, f32[64,256]{1,0:T(8,128)S(1)}, u32[]{:S(2)}, u32[]{:S(2)}) collective-permute-start(f32[64,256]{1,0:T(8,128)S(1)} %copy-done), channel_id=1, source_target_pairs={{16,0},{18,2},{20,4},{22,6},{24,8},{26,10},{28,12},{30,14},{0,16},... | collective-permute-start | bytes 196616 | tf_op jit(solution)/shard_map/ppermute | solution.py:14
  93.9 0.7 copy-start.3
  94.6 196.6 %all-reduce.7.cloned.1.call-start = ((), (), s32[]{:S(2)}) async-start(), calls=%async_computation.3 | async-start | bytes 786432 | tf_op jit(solution)/shard_map/psum | solution.py:138
  147.7 1.1 copy-start.2
  149.1 3.6 copy-start.5
  150.2 9.2 %collective-permute-start.10 = (f32[64,128]{1,0:T(8,128)S(1)}, f32[64,128]{1,0:T(8,128)S(1)}, u32[]{:S(2)}, u32[]{:S(2)}) collective-permute-start(f32[64,128]{1,0:T(8,128)S(1)} %convolution_add_fusion.3), channel_id=1, source_target_pairs={{30,0},{0,2},{2,4},{4,6},{6,8},{8,10},{10,12},{12,14},{14,16},{16,... | collective-permute-start | bytes 98312 | tf_op jit(solution)/shard_map/ppermute | solution.py:14
  151.2 8.2 %collective-permute-start.11 = (f32[64,128]{1,0:T(8,128)S(1)}, f32[64,128]{1,0:T(8,128)S(1)}, u32[]{:S(2)}, u32[]{:S(2)}) collective-permute-start(f32[64,128]{1,0:T(8,128)S(1)} %convolution_add_fusion.2), channel_id=1, source_target_pairs={{28,0},{30,2},{0,4},{2,6},{4,8},{6,10},{8,12},{10,14},{12,16},{14,... | collective-permute-start | bytes 98312 | tf_op jit(solution)/shard_map/ppermute | solution.py:14
  152.9 6.5 %collective-permute-start.12 = (f32[64,128]{1,0:T(8,128)S(1)}, f32[64,128]{1,0:T(8,128)S(1)}, u32[]{:S(2)}, u32[]{:S(2)}) collective-permute-start(f32[64,128]{1,0:T(8,128)S(1)} %convolution_add_fusion.1), channel_id=1, source_target_pairs={{26,0},{28,2},{30,4},{0,6},{2,8},{4,10},{6,12},{8,14},{10,16},{12,... | collective-permute-start | bytes 98312 | tf_op jit(solution)/shard_map/ppermute | solution.py:14
  155.3 5.7 %collective-permute-start.13 = (f32[64,128]{1,0:T(8,128)S(1)}, f32[64,128]{1,0:T(8,128)S(1)}, u32[]{:S(2)}, u32[]{:S(2)}) collective-permute-start(f32[64,128]{1,0:T(8,128)S(1)} %get-tuple-element.26), channel_id=1, source_target_pairs={{24,0},{26,2},{28,4},{30,6},{0,8},{2,10},{4,12},{6,14},{8,16},{10,... | collective-permute-start | bytes 98312 | tf_op jit(solution)/shard_map/ppermute | solution.py:14
  155.9 5.2 %collective-permute-start.14 = (f32[64,128]{1,0:T(8,128)S(1)}, f32[64,128]{1,0:T(8,128)S(1)}, u32[]{:S(2)}, u32[]{:S(2)}) collective-permute-start(f32[64,128]{1,0:T(8,128)S(1)} %get-tuple-element.27), channel_id=1, source_target_pairs={{16,0},{18,2},{20,4},{22,6},{24,8},{26,10},{28,12},{30,14},{0,16},... | collective-permute-start | bytes 98312 | tf_op jit(solution)/shard_map/ppermute | solution.py:14
  161.3 193.7 %copy-start.4 = (f32[64,128]{1,0:T(8,128)}, f32[64,128]{1,0:T(8,128)S(1)}, u32[]{:S(2)}) copy-start(f32[64,128]{1,0:T(8,128)S(1)} %fusion.31) | copy-start | bytes 98308
  329.4 24.0 %copy-start.6 = (f32[256,128]{1,0:T(8,128)S(1)}, f32[256,128]{1,0:T(8,128)}, u32[]{:S(2)}) copy-start(f32[256,128]{1,0:T(8,128)} %get-tuple-element.22) | copy-start | bytes 393220
Sparse Core Ops, SparseCore 0:
  19.4 128.3 all-reduce.4
  162.5 128.7 all-reduce.6
Sparse Core Ops, SparseCore 1:
  94.7 10.7 reduce-scatter.1
where the time goes:
time: 364 us; the launch traced here: 363 us
  waiting for transfers between devices  183 us (50%)
  blocking collectives  57.9 us (16%)
  other arithmetic  56.6 us (16%)
  starting transfers between devices  23.3 us (6%)
  between operations  18.6 us (5%)
  matrix products  14.9 us (4%)
  local copies, waits for them, and re-layouts  8.57 us (2%)
    psum x1, waiting for transfers between devices, per_device(): gram_sum, projected = lax.psum((gram_part, projected_part), ('blk', 'row'))  129 us
    psum x1, waiting for transfers between devices, per_device(): pivot_feats = lax.psum(picked, ('blk', 'row'))  52.4 us
    another operation x6, other arithmetic, per_device(): factor = jnp.linalg.cholesky(gram)  34 us
    all_gather x6, blocking collectives, member_sweep(): arrived_feats = lax.all_gather(fetched[upper][0], 'row', axis=0, tiled=True)  30.5 us
    all_gather x6, blocking collectives, member_sweep(): lax.all_gather(fetched[upper][1], 'row', axis=0, tiled=True)  27.4 us
    ppermute x15, starting transfers between devices, shifted(): return lax.ppermute(block, axis, route)  23.2 us
    another operation x3, other arithmetic, per_device(): coefficients = jax.scipy.linalg.cho_solve((factor, True), projected)  19.7 us
  transfers between devices with their start and end apart: 18, of which 3 were waited for; matrix products, arithmetic and copies ran while one was open for 4% of the time, Pallas kernels for 0%

commit v1 on v0

--- a/solution.py
+++ b/solution.py
@@ -118,7 +118,8 @@
     offsets = pivots - flat_index * local_rows
     inside = (offsets >= 0) & (offsets < local_rows)
     picked = jnp.where(inside[:, None], features[jnp.clip(offsets, 0, local_rows - 1)], 0.0)
-    pivot_feats = lax.psum(picked, ("blk", "row"))
+    parts = lax.all_gather(picked, ("blk", "row"))
+    pivot_feats = jnp.sum(parts, axis=0)
     pivot_norms = jnp.sum(pivot_feats * pivot_feats, axis=1)
     cross = amplitude * kernel_tile(features, own_norms, pivot_feats, pivot_norms)
     gram_part = lax.dot_general(

time: 364 us -> 348 us (0.956)
  waiting for transfers between devices: 183 us -> 152 us
  matrix products: 14.9 us -> 24.3 us
  other arithmetic: 56.6 us -> 62.1 us
    psum x1 -> x0, waiting for transfers between devices: 52.4 us -> none  [per_device(): pivot_feats = lax.psum(picked, ('blk', 'row'))]
    all_gather x0 -> x1, waiting for transfers between devices: none -> 19.3 us  [per_device(): parts = lax.all_gather(picked, ('blk', 'row'))]
    reduce_sum x0 -> x1, other arithmetic: none -> 3.93 us  [per_device(): pivot_feats = jnp.sum(parts, axis=0)]
  transfers between devices with their start and end apart: 18 -> 18, of which waited for: 3 -> 5; matrix products, arithmetic and copies ran while one was open for 4% -> 6% of each run, Pallas kernels for 0% -> 0%
where the time goes in v1:
time: 348 us; the launch traced here: 347 us
  waiting for transfers between devices  152 us (44%)
  other arithmetic  62.1 us (18%)
  blocking collectives  60.7 us (17%)
  matrix products  24.3 us (7%)
  starting transfers between devices  20.9 us (6%)
  between operations  18.7 us (5%)
  local copies, waits for them, and re-layouts  8.01 us (2%)
    psum x1, waiting for transfers between devices, per_device(): gram_sum, projected = lax.psum((gram_part, projected_part), ('blk', 'row'))  128 us
    another operation x6, other arithmetic, per_device(): factor = jnp.linalg.cholesky(gram)  34.2 us
    all_gather x6, blocking collectives, member_sweep(): arrived_feats = lax.all_gather(fetched[upper][0], 'row', axis=0, tiled=True)  30.7 us
    all_gather x6, blocking collectives, member_sweep(): lax.all_gather(fetched[upper][1], 'row', axis=0, tiled=True)  30 us
    ppermute x15, starting transfers between devices, shifted(): return lax.ppermute(block, axis, route)  20.8 us
    another operation x3, other arithmetic, per_device(): coefficients = jax.scipy.linalg.cho_solve((factor, True), projected)  19.7 us
    all_gather x1, waiting for transfers between devices, per_device(): parts = lax.all_gather(picked, ('blk', 'row'))  19.3 us
    dot_general x11, matrix products, kernel_tile(): lax.dot_general(row_feats, col_feats, (((1,), (1,)), ((), ())), precision...  7.9 us
  transfers between devices with their start and end apart: 18, of which 5 were waited for; matrix products, arithmetic and copies ran while one was open for 6% of the time, Pallas kernels for 0%

profile of v1, /device:TPU:0, one launch (start us, length us, event | category | flops | bytes accessed | tf_op | source)
XLA Modules:
  0.0 346.6 jit_solution(14330757230509133230)
XLA Ops:
  8.1 5.5 %collective-permute-start = (f32[64,256]{1,0:T(8,128)}, f32[64,256]{1,0:T(8,128)S(1)}, u32[]{:S(2)}, u32[]{:S(2)}) collective-permute-start(f32[64,256]{1,0:T(8,128)} %param.5), channel_id=1, source_target_pairs={{2,0},{4,2},{6,4},{8,6},{10,8},{12,10},{14,12},{16,14},{18,16},{20... | collective-permute-start | bytes 196616 | tf_op jit(solution)/shard_map/ppermute | solution.py:14
  14.9 2.6 collective-permute-start.8
  18.5 2.0 collective-permute-start.3
  20.5 5.0 %all_gather.42 = f32[128,256]{1,0:T(8,128)S(1)} all-gather(f32[64,256]{1,0:T(8,128)S(1)} %collective-permute-done), channel_id=1, replica_groups=mesh['blk'=16,'row'=2] {'row'}, dimensions={0}, use_global_device_ids=true | all-gather | bytes 196608 | tf_op jit(solution)/shard_map/all_gather | solution.py:66
  25.7 5.1 %all_gather.44 = f32[128,256]{1,0:T(8,128)S(1)} all-gather(f32[64,256]{1,0:T(8,128)S(1)} %collective-permute-done.2), channel_id=1, replica_groups=mesh['blk'=16,'row'=2] {'row'}, dimensions={0}, use_global_device_ids=true | all-gather | bytes 196608 | tf_op jit(solution)/shard_map/all_gather | solution.py:66
  33.3 5.5 %all_gather.46 = f32[128,256]{1,0:T(8,128)S(1)} all-gather(f32[64,256]{1,0:T(8,128)S(1)} %collective-permute-done.4), channel_id=1, replica_groups=mesh['blk'=16,'row'=2] {'row'}, dimensions={0}, use_global_device_ids=true | all-gather | bytes 196608 | tf_op jit(solution)/shard_map/all_gather | solution.py:66
  39.0 1.1 exponential_multiply_fusion.4
  40.1 4.9 %all_gather.48 = f32[128,256]{1,0:T(8,128)S(1)} all-gather(f32[64,256]{1,0:T(8,128)S(1)} %collective-permute-done.6), channel_id=1, replica_groups=mesh['blk'=16,'row'=2] {'row'}, dimensions={0}, use_global_device_ids=true | all-gather | bytes 196608 | tf_op jit(solution)/shard_map/all_gather | solution.py:66
  46.3 4.9 %all_gather.50 = f32[128,256]{1,0:T(8,128)S(1)} all-gather(f32[64,256]{1,0:T(8,128)S(1)} %collective-permute-done.8), channel_id=1, replica_groups=mesh['blk'=16,'row'=2] {'row'}, dimensions={0}, use_global_device_ids=true | all-gather | bytes 196608 | tf_op jit(solution)/shard_map/all_gather | solution.py:66
  59.3 1.8 gather_fusion
  62.8 3.4 collective-permute-start.7
  67.5 5.6 %all_gather.41 = f32[128,128]{1,0:T(8,128)S(1)} all-gather(f32[64,128]{1,0:T(8,128)} %param.6), channel_id=1, replica_groups=mesh['blk'=16,'row'=2] {'row'}, dimensions={0}, use_global_device_ids=true | all-gather | bytes 98304 | tf_op jit(solution)/shard_map/all_gather | solution.py:67
  73.0 5.1 %all_gather.40 = f32[128,256]{1,0:T(8,128)S(1)} all-gather(f32[64,256]{1,0:T(8,128)} %param.5), channel_id=1, replica_groups=mesh['blk'=16,'row'=2] {'row'}, dimensions={0}, use_global_device_ids=true | all-gather | bytes 196608 | tf_op jit(solution)/shard_map/all_gather | solution.py:66
  78.8 4.6 %all_gather.43 = f32[128,128]{1,0:T(8,128)S(1)} all-gather(f32[64,128]{1,0:T(8,128)S(1)} %collective-permute-done.1), channel_id=1, replica_groups=mesh['blk'=16,'row'=2] {'row'}, dimensions={0}, use_global_device_ids=true | all-gather | bytes 98304 | tf_op jit(solution)/shard_map/all_gather | solution.py:67
  83.4 4.6 %all_gather.47 = f32[128,128]{1,0:T(8,128)S(1)} all-gather(f32[64,128]{1,0:T(8,128)S(1)} %collective-permute-done.5), channel_id=1, replica_groups=mesh['blk'=16,'row'=2] {'row'}, dimensions={0}, use_global_device_ids=true | all-gather | bytes 98304 | tf_op jit(solution)/shard_map/all_gather | solution.py:67
  87.9 5.9 %all_gather.45 = f32[128,128]{1,0:T(8,128)S(1)} all-gather(f32[64,128]{1,0:T(8,128)S(1)} %collective-permute-done.3), channel_id=1, replica_groups=mesh['blk'=16,'row'=2] {'row'}, dimensions={0}, use_global_device_ids=true | all-gather | bytes 98304 | tf_op jit(solution)/shard_map/all_gather | solution.py:67
  93.8 4.7 %all_gather.51 = f32[128,128]{1,0:T(8,128)S(1)} all-gather(f32[64,128]{1,0:T(8,128)S(1)} %collective-permute-done.9), channel_id=1, replica_groups=mesh['blk'=16,'row'=2] {'row'}, dimensions={0}, use_global_device_ids=true | all-gather | bytes 98304 | tf_op jit(solution)/shard_map/all_gather | solution.py:67
  98.6 4.6 %all_gather.49 = f32[128,128]{1,0:T(8,128)S(1)} all-gather(f32[64,128]{1,0:T(8,128)S(1)} %collective-permute-done.7), channel_id=1, replica_groups=mesh['blk'=16,'row'=2] {'row'}, dimensions={0}, use_global_device_ids=true | all-gather | bytes 98304 | tf_op jit(solution)/shard_map/all_gather | solution.py:67
  109.2 4.3 %collective-permute-start.14 = (f32[64,128]{1,0:T(8,128)S(1)}, f32[64,128]{1,0:T(8,128)S(1)}, u32[]{:S(2)}, u32[]{:S(2)}) collective-permute-start(f32[64,128]{1,0:T(8,128)S(1)} %get-tuple-element.35), channel_id=1, source_target_pairs={{16,0},{18,2},{20,4},{22,6},{24,8},{26,10},{28,12},{30,14},{0,16},... | collective-permute-start | bytes 98312 | tf_op jit(solution)/shard_map/ppermute | solution.py:14
  114.0 1.9 collective-permute-done.13
  115.9 2.5 collective-permute-done.14
  119.4 19.3 %all-gather.2.cloned.1.call-done = f32[32,256,256]{2,1,0:T(8,128)} async-done(((f32[1,256,256]{2,1,0:T(8,128)}), f32[32,256,256]{2,1,0:T(8,128)}) %all-gather.2.cloned.1.call-update) | async-done | bytes 8388624 | tf_op jit(solution)/shard_map/all_gather | solution.py:121
  138.7 3.9 %reduce_sum.122 = f32[256,256]{1,0:T(8,128)S(1)} reduce(f32[32,256,256]{2,1,0:T(8,128)} %all-gather.2.cloned.1.call-done, f32[]{:T(128)} %constant.123.clone.1), dimensions={0}, to_apply=%region_11.0 | reduce | flops 2031616 | bytes 8650756 | tf_op jit(solution)/shard_map/reduce_sum | solution.py:122
  145.3 127.8 %all-reduce.4.cloned.1.call-done = (f32[256,128]{1,0:T(8,128)}, f32[256,256]{0,1:T(8,128)}) async-done(((f32[256,128]{1,0:T(8,128)}, f32[256,256]{0,1:T(8,128)}), (f32[256,128]{1,0:T(8,128)}, f32[256,256]{0,1:T(8,128)})) %all-reduce.4.cloned.1.call-update) | async-done | bytes 393232 | tf_op jit(solution)/shard_map/psum | solution.py:139
  273.1 1.5 multiply_add_fusion
  274.8 11.7 %cholesky.49 = f32[128,128]{1,0:T(8,128)S(1)} custom-call(f32[128,128]{1,0:T(8,128)S(1)} %cholesky.115), custom_call_target="Cholesky" | custom-call | tf_op jit(solution)/shard_map/jit(cholesky)/cholesky | solution.py:142
  286.6 9.8 %custom-call.18 = f32[1,128,128]{1,2,0:T(8,128)S(1)} custom-call(f32[1,128,128]{2,1,0:T(8,128)S(1)} %get-tuple-element.37), custom_call_target="InvertDiagBlocksLowerTriangular" | custom-call | tf_op jit(solution)/shard_map/jit(cholesky)/cholesky | solution.py:142
  296.9 11.9 %cholesky.103 = f32[128,128]{1,0:T(8,128)S(1)} custom-call(f32[128,128]{1,0:T(8,128)S(1)} %convolution_subtract_fusion.2), custom_call_target="Cholesky" | custom-call | tf_op jit(solution)/shard_map/jit(cholesky)/cholesky | solution.py:142
  311.2 4.2 %while.1 = (s32[]{:T(128)}, f32[256,256]{0,1:T(8,128)S(1)}, s32[2,2]{1,0:T(2,128)S(1)}, f32[2,128,128]{2,1,0:T(8,128)S(1)}, s32[]{:T(128)}) while((s32[]{:T(128)}, f32[256,256]{0,1:T(8,128)S(1)}, s32[2,2]{1,0:T(2,128)S(1)}, f32[2,128,128]{2,1,0:T(8,128)S(1)}, s32[]{:T(128)}) %tuple.29), condition=%wide.while_cond, body=%wide.while_body.sunk | while | flops 2 | bytes 393321 | solution.py:143
  311.8 1.4 dynamic-slice.7
  313.9 1.4 dynamic-slice.7
  315.4 19.7 %custom-call.19 = f32[2,128,128]{1,2,0:T(8,128)S(1)} custom-call(f32[2,128,128]{2,1,0:T(8,128)S(1)} %get-tuple-element.9), custom_call_target="InvertDiagBlocksLowerTriangular" | custom-call | tf_op jit(solution)/shard_map/jit(_cho_solve)/triangular_solve | solution.py:143
  (115 shorter events, 33.7 us)
Async XLA Ops:
  8.0 70.3 %copy-start = (f32[64,256]{1,0:T(8,128)S(1)}, f32[64,256]{1,0:T(8,128)}, u32[]{:S(2)}) copy-start(f32[64,256]{1,0:T(8,128)} %param.5) | copy-start | bytes 196612
  8.0 110.4 %copy-start.1 = (f32[64,128]{1,0:T(8,128)S(1)}, f32[64,128]{1,0:T(8,128)}, u32[]{:S(2)}) copy-start(f32[64,128]{1,0:T(8,128)} %param.6) | copy-start | bytes 98308
  8.0 96.1 %reduce-scatter.2.cloned.1.call-start = ((), (), s32[]{:S(2)}) async-start(), calls=%async_computation.1 | async-start | bytes 589824 | tf_op jit(solution)/shard_map/reduce_scatter | solution.py:111
  8.1 10.4 %collective-permute-start = (f32[64,256]{1,0:T(8,128)}, f32[64,256]{1,0:T(8,128)S(1)}, u32[]{:S(2)}, u32[]{:S(2)}) collective-permute-start(f32[64,256]{1,0:T(8,128)} %param.5), channel_id=1, source_target_pairs={{2,0},{4,2},{6,4},{8,6},{10,8},{12,10},{14,12},{16,14},{18,16},{20... | collective-permute-start | bytes 196616 | tf_op jit(solution)/shard_map/ppermute | solution.py:14
  13.6 12.1 %collective-permute-start.2 = (f32[64,256]{1,0:T(8,128)}, f32[64,256]{1,0:T(8,128)S(1)}, u32[]{:S(2)}, u32[]{:S(2)}) collective-permute-start(f32[64,256]{1,0:T(8,128)} %param.5), channel_id=1, source_target_pairs={{4,0},{6,2},{8,4},{10,6},{12,8},{14,10},{16,12},{18,14},{20,16},{2... | collective-permute-start | bytes 196616 | tf_op jit(solution)/shard_map/ppermute | solution.py:14
  14.2 19.1 %collective-permute-start.4 = (f32[64,256]{1,0:T(8,128)}, f32[64,256]{1,0:T(8,128)S(1)}, u32[]{:S(2)}, u32[]{:S(2)}) collective-permute-start(f32[64,256]{1,0:T(8,128)} %param.5), channel_id=1, source_target_pairs={{6,0},{8,2},{10,4},{12,6},{14,8},{16,10},{18,12},{20,14},{22,16},{... | collective-permute-start | bytes 196616 | tf_op jit(solution)/shard_map/ppermute | solution.py:14
  14.4 25.7 %collective-permute-start.6 = (f32[64,256]{1,0:T(8,128)}, f32[64,256]{1,0:T(8,128)S(1)}, u32[]{:S(2)}, u32[]{:S(2)}) collective-permute-start(f32[64,256]{1,0:T(8,128)} %param.5), channel_id=1, source_target_pairs={{8,0},{10,2},{12,4},{14,6},{16,8},{18,10},{20,12},{22,14},{24,16},... | collective-permute-start | bytes 196616 | tf_op jit(solution)/shard_map/ppermute | solution.py:14
  14.9 31.4 %collective-permute-start.8 = (f32[64,256]{1,0:T(8,128)}, f32[64,256]{1,0:T(8,128)S(1)}, u32[]{:S(2)}, u32[]{:S(2)}) collective-permute-start(f32[64,256]{1,0:T(8,128)} %param.5), channel_id=1, source_target_pairs={{16,0},{18,2},{20,4},{22,6},{24,8},{26,10},{28,12},{30,14},{0,16},... | collective-permute-start | bytes 196616 | tf_op jit(solution)/shard_map/ppermute | solution.py:14
  18.5 38.4 %collective-permute-start.3 = (f32[64,128]{1,0:T(8,128)}, f32[64,128]{1,0:T(8,128)S(1)}, u32[]{:S(2)}, u32[]{:S(2)}) collective-permute-start(f32[64,128]{1,0:T(8,128)} %param.6), channel_id=1, source_target_pairs={{4,0},{6,2},{8,4},{10,6},{12,8},{14,10},{16,12},{18,14},{20,16},{2... | collective-permute-start | bytes 98312 | tf_op jit(solution)/shard_map/ppermute | solution.py:14
  25.7 31.5 %collective-permute-start.1 = (f32[64,128]{1,0:T(8,128)}, f32[64,128]{1,0:T(8,128)S(1)}, u32[]{:S(2)}, u32[]{:S(2)}) collective-permute-start(f32[64,128]{1,0:T(8,128)} %param.6), channel_id=1, source_target_pairs={{2,0},{4,2},{6,4},{8,6},{10,8},{12,10},{14,12},{16,14},{18,16},{20... | collective-permute-start | bytes 98312 | tf_op jit(solution)/shard_map/ppermute | solution.py:14
  33.3 24.2 %collective-permute-start.5 = (f32[64,128]{1,0:T(8,128)}, f32[64,128]{1,0:T(8,128)S(1)}, u32[]{:S(2)}, u32[]{:S(2)}) collective-permute-start(f32[64,128]{1,0:T(8,128)} %param.6), channel_id=1, source_target_pairs={{6,0},{8,2},{10,4},{12,6},{14,8},{16,10},{18,12},{20,14},{22,16},{... | collective-permute-start | bytes 98312 | tf_op jit(solution)/shard_map/ppermute | solution.py:14
  57.8 0.8 copy-start.2
  58.6 80.1 %all-gather.2.cloned.1.call-start = ((), (), s32[]{:S(2)}) async-start(), calls=%async_computation.2 | async-start | bytes 8650752 | tf_op jit(solution)/shard_map/all_gather | solution.py:121
  62.7 210.4 %all-reduce.4.cloned.1.call-start = ((), (), s32[]{:S(2)}) async-start(), calls=%async_computation.3 | async-start | bytes 786432 | tf_op jit(solution)/shard_map/psum | solution.py:139
  62.7 31.1 %collective-permute-start.9 = (f32[64,128]{1,0:T(8,128)}, f32[64,128]{1,0:T(8,128)S(1)}, u32[]{:S(2)}, u32[]{:S(2)}) collective-permute-start(f32[64,128]{1,0:T(8,128)} %param.6), channel_id=1, source_target_pairs={{16,0},{18,2},{20,4},{22,6},{24,8},{26,10},{28,12},{30,14},{0,16},... | collective-permute-start | bytes 98312 | tf_op jit(solution)/shard_map/ppermute | solution.py:14
  62.8 35.8 %collective-permute-start.7 = (f32[64,128]{1,0:T(8,128)}, f32[64,128]{1,0:T(8,128)S(1)}, u32[]{:S(2)}, u32[]{:S(2)}) collective-permute-start(f32[64,128]{1,0:T(8,128)} %param.6), channel_id=1, source_target_pairs={{8,0},{10,2},{12,4},{14,6},{16,8},{18,10},{20,12},{22,14},{24,16},... | collective-permute-start | bytes 98312 | tf_op jit(solution)/shard_map/ppermute | solution.py:14
  105.1 8.6 %collective-permute-start.10 = (f32[64,128]{1,0:T(8,128)S(1)}, f32[64,128]{1,0:T(8,128)S(1)}, u32[]{:S(2)}, u32[]{:S(2)}) collective-permute-start(f32[64,128]{1,0:T(8,128)S(1)} %convolution_add_fusion.3), channel_id=1, source_target_pairs={{30,0},{0,2},{2,4},{4,6},{6,8},{8,10},{10,12},{12,14},{14,16},{16,... | collective-permute-start | bytes 98312 | tf_op jit(solution)/shard_map/ppermute | solution.py:14
  106.1 7.6 %collective-permute-start.11 = (f32[64,128]{1,0:T(8,128)S(1)}, f32[64,128]{1,0:T(8,128)S(1)}, u32[]{:S(2)}, u32[]{:S(2)}) collective-permute-start(f32[64,128]{1,0:T(8,128)S(1)} %convolution_add_fusion.2), channel_id=1, source_target_pairs={{28,0},{30,2},{0,4},{2,6},{4,8},{6,10},{8,12},{10,14},{12,16},{14,... | collective-permute-start | bytes 98312 | tf_op jit(solution)/shard_map/ppermute | solution.py:14
  107.1 6.9 %collective-permute-start.12 = (f32[64,128]{1,0:T(8,128)S(1)}, f32[64,128]{1,0:T(8,128)S(1)}, u32[]{:S(2)}, u32[]{:S(2)}) collective-permute-start(f32[64,128]{1,0:T(8,128)S(1)} %convolution_add_fusion.1), channel_id=1, source_target_pairs={{26,0},{28,2},{30,4},{0,6},{2,8},{4,10},{6,12},{8,14},{10,16},{12,... | collective-permute-start | bytes 98312 | tf_op jit(solution)/shard_map/ppermute | solution.py:14
  108.4 7.5 %collective-permute-start.13 = (f32[64,128]{1,0:T(8,128)S(1)}, f32[64,128]{1,0:T(8,128)S(1)}, u32[]{:S(2)}, u32[]{:S(2)}) collective-permute-start(f32[64,128]{1,0:T(8,128)S(1)} %get-tuple-element.34), channel_id=1, source_target_pairs={{24,0},{26,2},{28,4},{30,6},{0,8},{2,10},{4,12},{6,14},{8,16},{10,... | collective-permute-start | bytes 98312 | tf_op jit(solution)/shard_map/ppermute | solution.py:14
  109.2 9.2 %collective-permute-start.14 = (f32[64,128]{1,0:T(8,128)S(1)}, f32[64,128]{1,0:T(8,128)S(1)}, u32[]{:S(2)}, u32[]{:S(2)}) collective-permute-start(f32[64,128]{1,0:T(8,128)S(1)} %get-tuple-element.35), channel_id=1, source_target_pairs={{16,0},{18,2},{20,4},{22,6},{24,8},{26,10},{28,12},{30,14},{0,16},... | collective-permute-start | bytes 98312 | tf_op jit(solution)/shard_map/ppermute | solution.py:14
  119.4 218.9 %copy-start.3 = (f32[64,128]{1,0:T(8,128)}, f32[64,128]{1,0:T(8,128)S(1)}, u32[]{:S(2)}) copy-start(f32[64,128]{1,0:T(8,128)S(1)} %fusion.31) | copy-start | bytes 98308
Sparse Core Ops, SparseCore 0:
  58.7 11.2 reduce-scatter.1
Sparse Core Ops, SparseCore 1:
  62.7 75.9 all-gather.1
  145.4 127.7 all-reduce.3
